TPU v7x, 256 devices: a whole 4x4x8 slice. The times are simulated.
256 devices in a mesh: layer: 4 (over y), row: 8 (over x, z_lo), col: 8 (over z_hi, core).
Axes of the slice: x: 4, y: 4, z: 8 (z_hi: 4, z_lo: 2; z = z_hi * 2 + z_lo), core: 2. Of those that a mesh axis runs over, the one named last changes fastest.
Arguments:
- ancestor: float32 [8192, 8192], P('row', 'col'), may hold values from -768 to 3840, as said below
- coupling: bfloat16 [4, 8192, 1024], P('layer', ('row', 'col')), may hold values from -10 to 10
- fronts: float32 [4, 2, 512, 512], P('layer', None, None, ('row', 'col')), may hold values from -10 to 360, as said below
- tile_pattern: int32 [4, 2, 8], P('layer'), may hold values 0 or 1
Outputs:
- schur: float32 [8192, 8192], P('row', 'col')
- panel_factor: float32 [8192, 512], P(('row', 'col'))
- pivots: float32 [512], P(('row', 'col'))
Inputs may be any that keep to these rules, and one draw needn't show every extreme that they name: `ancestor`: symmetric and positive definite; the leading [512, 512] block of schur_0 stays positive definite after all layers' terms are subtracted. `fronts`: each [512, 512] block is symmetric and positive definite, with diagonal entries from 200 to 360 and other entries within -10 to 10.
All inputs are finite; a program needn't handle non-finite values. No bound on the sum of `tile_pattern` on one device may be relied on, other than what follows from the above.
Results may differ from a plain program's by a relative error of at most 0.0008.
Values may be sent and summed in bfloat16 or wider, within the bound.
A program may use at most 128 MiB of HBM per device.

v0:
```python
import jax
import jax.numpy as jnp
from jax import lax
from jax.sharding import PartitionSpec as P

S = 8192
TILE = 1024
P_SIZE = 512
NP = 2


def spread(value, axis, source):
    kept = jnp.where(lax.axis_index(axis) == source, value, 0).astype(value.dtype)
    return lax.psum(kept, axis)


def filled_up(lines, size):
    spare = -len(lines) % size
    return jnp.pad(lines, [(0, spare)] + [(0, 0)] * (lines.ndim - 1))


def spread_2(x, axis, root):
    lines = jnp.where(lax.axis_index(axis) == root, x, jnp.zeros_like(x)).reshape(
        -1, *x.shape[1:][-1:]
    )
    padded = filled_up(lines, lax.axis_size(axis))
    own = lax.psum_scatter(padded, axis, scatter_dimension=0, tiled=True)
    return lax.all_gather(own, axis, axis=0, tiled=True)[: len(lines)].reshape(x.shape)


def column_block(sender):
    row_count = lax.axis_size("row")
    col_count = lax.axis_size("col")
    col_place = lax.axis_index("col")
    first_root = col_place * row_count // col_count
    pieces = sender(first_root + 0)
    return pieces


def solve_rows(factor, columns):
    return lax.linalg.triangular_solve(
        factor, columns, left_side=False, lower=True, transpose_a=True
    )


def local(ancestor, coupling, fronts, tile_pattern):
    row_count = lax.axis_size("row")
    col_count = lax.axis_size("col")
    row_place = lax.axis_index("row")
    col_place = lax.axis_index("col")
    local_rows = S // (row_count * col_count)
    block_rows = S // row_count
    gathered = lax.all_gather(
        fronts.astype(jnp.bfloat16), ("row", "col"), axis=3, tiled=True
    ).astype(fronts.dtype)
    factors = jnp.linalg.cholesky(gathered[0])
    first_row = (row_place * col_count + col_place) * local_rows
    positions = first_row + lax.iota(jnp.int32, local_rows)
    onehot = (positions[:, None] // TILE == lax.iota(jnp.int32, S // TILE)[None, :]).astype(
        jnp.float32
    )
    row_masks = jnp.dot(onehot, tile_pattern[0].T.astype(jnp.float32))
    solved_parts = []
    for panel in range(NP):
        columns = (
            coupling[0, :, panel * P_SIZE : (panel + 1) * P_SIZE].astype(jnp.float32)
            * row_masks[:, panel : panel + 1]
        )
        solved_parts.append(solve_rows(factors[panel], columns))
    scaled = jnp.concatenate(solved_parts, 1).astype(jnp.bfloat16)
    row_side = lax.all_gather(scaled, "col", axis=0, tiled=True)
    col_side = column_block(lambda source: spread(row_side, "row", source))
    update = -lax.dot_general(
        row_side, col_side, (((1,), (1,)), ((), ())), preferred_element_type=jnp.float32
    )
    shared = lax.psum_scatter(
        update.astype(jnp.bfloat16), "layer", scatter_dimension=0, tiled=True
    ).astype(jnp.float32)
    summed = lax.all_gather(shared.astype(jnp.bfloat16), "layer", axis=0, tiled=True).astype(
        shared.dtype
    )
    leading = ancestor[:, :P_SIZE] + summed[:, :P_SIZE]
    global_rows = row_place * block_rows + lax.iota(jnp.int32, block_rows)
    trailing = None
    working = leading
    pivot_source = working[0:P_SIZE, 0:P_SIZE]
    pivot_block = spread(pivot_source, ("row", "col"), 0)
    pivot_chol = jnp.linalg.cholesky(pivot_block)
    keep_rows = (global_rows >= 0)[:, None]
    received = spread_2(working, "col", 0)
    solved = solve_rows(pivot_chol, received)
    panel_rows = jnp.where(keep_rows, solved, jnp.zeros_like(solved))
    panel_cols = column_block(lambda source: spread(panel_rows, "row", source))
    leading = leading - jnp.dot(
        panel_rows,
        panel_cols[:P_SIZE].T,
        precision=lax.Precision.HIGHEST,
        preferred_element_type=jnp.float32,
    )
    history = (panel_rows, panel_cols)
    panel_outs = lax.dynamic_slice_in_dim(panel_rows, col_place * local_rows, local_rows, 0)
    diagonal = jnp.diagonal(pivot_chol)
    pivot_outs = diagonal * diagonal
    trailing = ancestor[:, P_SIZE:] + summed[:, P_SIZE:]
    rows_part, cols_part = history
    trailing = trailing - jnp.dot(
        rows_part,
        cols_part[P_SIZE:].T,
        precision=lax.Precision.HIGHEST,
        preferred_element_type=jnp.float32,
    )
    schur = jnp.concatenate([leading, trailing], 1)
    pivot_share = pivot_outs.shape[0] // (row_count * col_count)
    flat_place = row_place * col_count + col_place
    my_pivots = lax.dynamic_slice_in_dim(pivot_outs, flat_place * pivot_share, pivot_share, 0)
    return (schur, panel_outs, my_pivots)


def solution(mesh):
    return jax.shard_map(
        local,
        mesh=mesh,
        in_specs=(
            P("row", "col"),
            P("layer", ("row", "col"), None),
            P("layer", None, None, ("row", "col")),
            P("layer", None, None),
        ),
        out_specs=(P("row", "col"), P(("row", "col"), None), P(("row", "col"))),
        check_vma=False,
    )
```

profile of v0, /device:TPU:1, one launch (start us, length us, event | category | flops | bytes accessed | tf_op | source)
XLA Modules:
  0.0 1092.7 jit_solution(2963737448343294521)
XLA Ops:
  12.0 115.7 %all-gather.5.cloned.1.call-done = bf16[1,2,512,512]{2,3,1,0:T(8,128)(2,1)} async-done(((bf16[1,2,512,8]{2,3,1,0:T(8,128)(2,1)}), bf16[1,2,512,512]{2,3,1,0:T(8,128)(2,1)}) %all-gather.5.cloned.1.call-update) | async-done | bytes 1048592 | tf_op jit(solution)/shard_map/all_gather | solution.py:53
  134.3 23.5 %custom-call.64 = f32[2,128,128]{2,1,0:T(8,128)S(1)} custom-call(f32[2,128,128]{2,1,0:T(8,128)S(1)} %cholesky.531), custom_call_target="Cholesky" | custom-call | tf_op jit(solution)/shard_map/jit(cholesky)/cholesky | solution.py:56
  157.8 19.7 %custom-call.65 = f32[2,1,128,128]{2,3,1,0:T(8,128)S(1)} custom-call(f32[2,1,128,128]{3,2,1,0:T(8,128)S(1)} %select_bitcast_fusion.2), custom_call_target="InvertDiagBlocksLowerTriangular" | custom-call | tf_op jit(solution)/shard_map/jit(cholesky)/cholesky | solution.py:56
  180.7 23.5 %custom-call.66 = f32[2,128,128]{2,1,0:T(8,128)S(1)} custom-call(f32[2,128,128]{2,1,0:T(8,128)S(1)} %cholesky.535), custom_call_target="Cholesky" | custom-call | tf_op jit(solution)/shard_map/jit(cholesky)/cholesky | solution.py:56
  204.2 19.8 %custom-call.67 = f32[2,1,128,128]{2,3,1,0:T(8,128)S(1)} custom-call(f32[2,1,128,128]{3,2,1,0:T(8,128)S(1)} %get-tuple-element.98), custom_call_target="InvertDiagBlocksLowerTriangular" | custom-call | tf_op jit(solution)/shard_map/jit(cholesky)/cholesky | solution.py:56
  226.1 23.5 %custom-call.68 = f32[2,128,128]{2,1,0:T(8,128)S(1)} custom-call(f32[2,128,128]{2,1,0:T(8,128)S(1)} %cholesky.540), custom_call_target="Cholesky" | custom-call | tf_op jit(solution)/shard_map/jit(cholesky)/cholesky | solution.py:56
  249.5 19.7 %custom-call.69 = f32[2,1,128,128]{2,3,1,0:T(8,128)S(1)} custom-call(f32[2,1,128,128]{3,2,1,0:T(8,128)S(1)} %get-tuple-element.96), custom_call_target="InvertDiagBlocksLowerTriangular" | custom-call | tf_op jit(solution)/shard_map/jit(cholesky)/cholesky | solution.py:56
  271.0 23.7 %custom-call.70 = f32[2,128,128]{2,1,0:T(8,128)S(1)} custom-call(f32[2,128,128]{2,1,0:T(8,128)S(1)} %convolution_subtract_fusion.7), custom_call_target="Cholesky" | custom-call | tf_op jit(solution)/shard_map/jit(cholesky)/cholesky | solution.py:56
  295.8 8.5 while.6
  304.2 39.3 %custom-call.78 = f32[4,128,128]{1,2,0:T(8,128)S(1)} custom-call(f32[4,128,128]{2,1,0:T(8,128)S(1)} %get-tuple-element.26), custom_call_target="InvertDiagBlocksLowerTriangular" | custom-call | tf_op jit(solution)/shard_map/triangular_solve/custom-call.14 | solution.py:41
  343.6 8.5 while.7
  352.1 39.7 %custom-call.79 = f32[4,128,128]{1,2,0:T(8,128)S(1)} custom-call(f32[4,128,128]{2,1,0:T(8,128)S(1)} %get-tuple-element.27), custom_call_target="InvertDiagBlocksLowerTriangular" | custom-call | tf_op jit(solution)/shard_map/triangular_solve/custom-call.14 | solution.py:41
  397.4 38.6 %all-gather.7.cloned.1.call-done = bf16[1024,1024]{0,1:T(8,128)(2,1)} async-done(((bf16[128,1024]{0,1:T(8,128)(2,1)}), bf16[1024,1024]{0,1:T(8,128)(2,1)}) %all-gather.7.cloned.1.call-update) | async-done | bytes 2097168 | tf_op jit(solution)/shard_map/all_gather | solution.py:71
  437.6 108.4 %all-reduce.6.cloned.1.call-done = bf16[1024,1024]{0,1:T(8,128)(2,1)} async-done(((bf16[1024,1024]{0,1:T(8,128)(2,1)}), bf16[1024,1024]{0,1:T(8,128)(2,1)}) %all-reduce.6.cloned.1.call-update) | async-done | bytes 2097168 | tf_op jit(solution)/shard_map/psum | solution.py:14
  546.0 5.3 negate_convert_fusion
  551.4 32.3 %reduce-scatter.3.cloned.1.call-done = bf16[256,1024]{0,1:T(8,128)(2,1)} async-done(((bf16[1024,1024]{0,1:T(8,128)(2,1)}), bf16[256,1024]{0,1:T(8,128)(2,1)}) %reduce-scatter.3.cloned.1.call-update) | async-done | bytes 524304 | tf_op jit(solution)/shard_map/reduce_scatter | solution.py:76
  590.4 29.9 %all-gather.9.cloned.1.call-done = bf16[1024,1024]{0,1:T(8,128)(2,1)} async-done(((bf16[256,1024]{0,1:T(8,128)(2,1)}), bf16[1024,1024]{0,1:T(8,128)(2,1)}) %all-gather.9.cloned.1.call-update) | async-done | bytes 2097168 | tf_op jit(solution)/shard_map/all_gather | solution.py:79
  628.4 186.2 %all-reduce.8.cloned.1.call-done = f32[512,512]{0,1:T(8,128)} async-done(((f32[512,512]{0,1:T(8,128)}), f32[512,512]{0,1:T(8,128)}) %all-reduce.8.cloned.1.call-update) | async-done | bytes 1048592 | tf_op jit(solution)/shard_map/psum | solution.py:14
  816.5 11.7 %cholesky.467 = f32[128,128]{1,0:T(8,128)S(1)} custom-call(f32[128,128]{1,0:T(8,128)S(1)} %cholesky.544), custom_call_target="Cholesky" | custom-call | tf_op jit(solution)/shard_map/jit(cholesky)/cholesky | solution.py:88
  828.4 9.8 custom-call.71
  839.0 11.7 %cholesky.483 = f32[128,128]{1,0:T(8,128)S(1)} custom-call(f32[128,128]{1,0:T(8,128)S(1)} %cholesky.548), custom_call_target="Cholesky" | custom-call | tf_op jit(solution)/shard_map/jit(cholesky)/cholesky | solution.py:88
  850.8 10.0 custom-call.72
  862.0 11.7 %cholesky.504 = f32[128,128]{1,0:T(8,128)S(1)} custom-call(f32[128,128]{1,0:T(8,128)S(1)} %cholesky.553), custom_call_target="Cholesky" | custom-call | tf_op jit(solution)/shard_map/jit(cholesky)/cholesky | solution.py:88
  873.9 9.8 custom-call.73
  884.5 11.7 %cholesky.521 = f32[128,128]{1,0:T(8,128)S(1)} custom-call(f32[128,128]{1,0:T(8,128)S(1)} %convolution_subtract_fusion.12), custom_call_target="Cholesky" | custom-call | tf_op jit(solution)/shard_map/jit(cholesky)/cholesky | solution.py:88
  901.8 8.6 while.5
  910.3 39.3 %custom-call.74 = f32[4,128,128]{1,2,0:T(8,128)S(1)} custom-call(f32[4,128,128]{2,1,0:T(8,128)S(1)} %get-tuple-element.19), custom_call_target="InvertDiagBlocksLowerTriangular" | custom-call | tf_op jit(solution)/shard_map/triangular_solve | solution.py:41
  961.9 4.7 gather_fusion
  968.1 99.3 %all-reduce.10.cloned.1.call-done = f32[1024,512]{0,1:T(8,128)} async-done(((f32[1024,512]{0,1:T(8,128)}), f32[1024,512]{0,1:T(8,128)}) %all-reduce.10.cloned.1.call-update) | async-done | bytes 2097168 | tf_op jit(solution)/shard_map/psum | solution.py:14
  1067.5 5.7 convolution_subtract_fusion
  1073.2 5.0 fusion
  1080.6 5.3 copy.74
  (191 shorter events, 90.0 us)
Async XLA Ops:
  7.2 120.6 %all-gather.5.cloned.1.call-start = ((), (), s32[]{:S(2)}) async-start(), calls=%async_computation.2 | async-start | bytes 1064960 | tf_op jit(solution)/shard_map/all_gather | solution.py:53
  8.6 427.5 %all-gather.7.cloned.1.call-start = ((), (), s32[]{:S(2)}) async-start(), calls=%async_computation.3 | async-start | bytes 2359296 | tf_op jit(solution)/shard_map/all_gather | solution.py:71
  130.6 2.0 copy-start.5
  132.9 1.3 copy-start.4
  295.7 96.1 %copy-start.10 = (f32[128,512]{1,0:T(8,128)S(1)}, f32[128,512]{1,0:T(8,128)}, u32[]{:S(2)}) copy-start(f32[128,512]{1,0:T(8,128)} %get-tuple-element.93) | copy-start | bytes 786436
  295.7 98.5 %copy-start.9 = (f32[128,512]{1,0:T(8,128)S(1)}, f32[128,512]{1,0:T(8,128)}, u32[]{:S(2)}) copy-start(f32[128,512]{1,0:T(8,128)} %get-tuple-element.94) | copy-start | bytes 786436
  397.4 148.6 %all-reduce.6.cloned.1.call-start = ((), (), s32[]{:S(2)}) async-start(), calls=%async_computation.4 | async-start | bytes 4194304 | tf_op jit(solution)/shard_map/psum | solution.py:14
  437.5 108.5 %copy-start.8 = (bf16[1024,1024]{0,1:T(8,128)(2,1)S(1)}, bf16[1024,1024]{0,1:T(8,128)(2,1)}, u32[]{:S(2)}) copy-start(bf16[1024,1024]{0,1:T(8,128)(2,1)} %all-gather.7.cloned.1.call-done) | copy-start | bytes 6291460
  437.5 146.1 %reduce-scatter.3.cloned.1.call-start = ((), (), s32[]{:S(2)}) async-start(), calls=%async_computation.5 | async-start | bytes 2621440 | tf_op jit(solution)/shard_map/reduce_scatter | solution.py:76
  551.3 69.0 %all-gather.9.cloned.1.call-start = ((), (), s32[]{:S(2)}) async-start(), calls=%async_computation.6 | async-start | bytes 2621440 | tf_op jit(solution)/shard_map/all_gather | solution.py:79
  583.7 230.9 %all-reduce.8.cloned.1.call-start = ((), (), s32[]{:S(2)}) async-start(), calls=%async_computation.9 | async-start | bytes 2097152 | tf_op jit(solution)/shard_map/psum | solution.py:14
  622.4 2.7 copy-start
  625.0 1.3 copy-start.2
  627.4 233.9 %reduce-scatter.5.cloned.1.call-start = ((), (), s32[]{:S(2)}) async-start(), calls=%async_computation.7 | async-start | bytes 2359296 | tf_op jit(solution)/shard_map/reduce_scatter | solution.py:27
  628.2 321.5 %all-gather.11.cloned.1.call-start = ((), (), s32[]{:S(2)}) async-start(), calls=%async_computation.8 | async-start | bytes 2359296 | tf_op jit(solution)/shard_map/all_gather | solution.py:28
  814.6 1.7 copy-start.6
  861.4 206.1 %all-reduce.10.cloned.1.call-start = ((), (), s32[]{:S(2)}) async-start(), calls=%async_computation.10 | async-start | bytes 4194304 | tf_op jit(solution)/shard_map/psum | solution.py:14
  949.7 4.1 copy-start.7
  1067.5 5.7 copy-start.1
  1067.5 5.7 copy-start.3
Sparse Core Ops, SparseCore 0:
  10.4 117.2 all-gather.4
  397.5 38.5 all-gather.6
  439.3 106.6 all-reduce.5
  551.5 32.1 reduce-scatter.2
  585.3 34.9 all-gather.8
  627.5 187.0 all-reduce.7
  817.2 42.0 reduce-scatter.4
  861.5 40.6 all-gather.10
  959.1 108.2 all-reduce.9
where the time goes:
time: 1100 us; the launch traced here: 1090 us
  waiting for transfers between devices  611 us (56%)
  other arithmetic  371 us (34%)
  local copies, waits for them, and re-layouts  53.8 us (5%)
  matrix products  37.8 us (3%)
  between operations  17.4 us (2%)
    psum x3, waiting for transfers between devices, spread(): return lax.psum(kept, axis)  394 us
    another operation x16, other arithmetic, local(): factors = jnp.linalg.cholesky(gathered[0])  154 us
    another operation x6, other arithmetic, solve_rows(): lax.linalg.triangular_solve(factor, columns, left_side=False, lower=True,...  119 us
    all_gather x1, waiting for transfers between devices, local(): lax.all_gather(fronts.astype(jnp.bfloat16), ('row', 'col'), axis=3, tiled...  116 us
    another operation x15, other arithmetic, local(): pivot_chol = jnp.linalg.cholesky(pivot_block)  79.2 us
    all_gather x1, waiting for transfers between devices, local(): row_side = lax.all_gather(scaled, 'col', axis=0, tiled=True)  38.6 us
    reduce_scatter x1, waiting for transfers between devices, local(): lax.psum_scatter(update.astype(jnp.bfloat16), 'layer', scatter_dimension=...  32.3 us
    all_gather x1, waiting for transfers between devices, local(): lax.all_gather(shared.astype(jnp.bfloat16), 'layer', axis=0, tiled=True)  29.9 us
  transfers between devices with their start and end apart: 9, of which 7 were waited for; matrix products, arithmetic and copies ran while one was open for 14% of the time, Pallas kernels for 0%

commit v1 on v0

--- a/solution.py
+++ b/solution.py
@@ -50,8 +50,14 @@
     col_place = lax.axis_index("col")
     local_rows = S // (row_count * col_count)
     block_rows = S // row_count
-    gathered = lax.all_gather(
-        fronts.astype(jnp.bfloat16), ("row", "col"), axis=3, tiled=True
+    gathered = jnp.concatenate(
+        lax.all_to_all(
+            jnp.stack([fronts.astype(jnp.bfloat16)] * lax.axis_size(("row", "col"))),
+            ("row", "col"),
+            0,
+            0,
+        ),
+        axis=3,
     ).astype(fronts.dtype)
     factors = jnp.linalg.cholesky(gathered[0])
     first_row = (row_place * col_count + col_place) * local_rows

time: 1100 us -> 1020 us (0.927)
  waiting for transfers between devices: 611 us -> 521 us
  starting transfers between devices: 0.53 us -> 13.5 us
    all_gather x1 -> x0, waiting for transfers between devices: 116 us -> none  [local(): lax.all_gather(fronts.astype(jnp.bfloat16), ('row', 'col'), axis=3, tiled...]
    all_to_all x0 -> x1, waiting for transfers between devices: none -> 26.2 us  [local(): lax.all_to_all(jnp.stack([fronts.astype(jnp.bfloat16)] * lax.axis_size(('...]
    all_to_all x0 -> x1, starting transfers between devices: none -> 13 us  [local(): lax.all_to_all(jnp.stack([fronts.astype(jnp.bfloat16)] * lax.axis_size(('...]
  transfers between devices with their start and end apart: 9 -> 9, of which waited for: 7 -> 7; matrix products, arithmetic and copies ran while one was open for 14% -> 15% of each run, Pallas kernels for 0% -> 0%
where the time goes in v1:
time: 1020 us; the launch traced here: 1010 us
  waiting for transfers between devices  521 us (51%)
  other arithmetic  368 us (36%)
  local copies, waits for them, and re-layouts  54.1 us (5%)
  matrix products  37.1 us (4%)
  between operations  17.7 us (2%)
  starting transfers between devices  13.5 us (1%)
    psum x3, waiting for transfers between devices, spread(): return lax.psum(kept, axis)  394 us
    another operation x16, other arithmetic, local(): factors = jnp.linalg.cholesky(gathered[0])  154 us
    another operation x6, other arithmetic, solve_rows(): lax.linalg.triangular_solve(factor, columns, left_side=False, lower=True,...  119 us
    another operation x15, other arithmetic, local(): pivot_chol = jnp.linalg.cholesky(pivot_block)  79.2 us
    all_gather x1, waiting for transfers between devices, local(): row_side = lax.all_gather(scaled, 'col', axis=0, tiled=True)  38.1 us
    reduce_scatter x1, waiting for transfers between devices, local(): lax.psum_scatter(update.astype(jnp.bfloat16), 'layer', scatter_dimension=...  32.3 us
    all_gather x1, waiting for transfers between devices, local(): lax.all_gather(shared.astype(jnp.bfloat16), 'layer', axis=0, tiled=True)  29.9 us
    all_to_all x1, waiting for transfers between devices, local(): lax.all_to_all(jnp.stack([fronts.astype(jnp.bfloat16)] * lax.axis_size(('...  26.2 us
  transfers between devices with their start and end apart: 9, of which 7 were waited for; matrix products, arithmetic and copies ran while one was open for 15% of the time, Pallas kernels for 0%

profile of v1, /device:TPU:1, one launch (start us, length us, event | category | flops | bytes accessed | tf_op | source)
XLA Modules:
  0.0 1012.7 jit_solution(285605418660654034)
XLA Ops:
  9.1 13.0 %all-to-all-start = ((bf16[64,1,2,512,8]{3,4,2,1,0:T(8,128)(2,1)}), bf16[64,1,2,512,8]{3,4,2,1,0:T(8,128)(2,1)S(1)}, u32[]{:S(2)}, u32[]{:S(2)}) async-start(bf16[64,1,2,512,8]{3,4,2,1,0:T(8,128)(2,1)} %stack.2), calls=%async_computation | async-start | bytes 2097152 | tf_op jit(solution)/shard_map/all_to_all | solution.py:54
  23.8 26.2 %all-to-all-done = bf16[64,1,2,512,8]{3,4,2,1,0:T(8,128)(2,1)S(1)} async-done(((bf16[64,1,2,512,8]{3,4,2,1,0:T(8,128)(2,1)}), bf16[64,1,2,512,8]{3,4,2,1,0:T(8,128)(2,1)S(1)}, u32[]{:S(2)}, u32[]{:S(2)}) %all-to-all-start) | async-done | bytes 1048608 | tf_op jit(solution)/shard_map/all_to_all | solution.py:54
  55.2 23.5 %custom-call.64 = f32[2,128,128]{2,1,0:T(8,128)S(1)} custom-call(f32[2,128,128]{2,1,0:T(8,128)S(1)} %cholesky.531), custom_call_target="Cholesky" | custom-call | tf_op jit(solution)/shard_map/jit(cholesky)/cholesky | solution.py:62
  78.7 19.7 %custom-call.65 = f32[2,1,128,128]{2,3,1,0:T(8,128)S(1)} custom-call(f32[2,1,128,128]{3,2,1,0:T(8,128)S(1)} %select_bitcast_fusion.2), custom_call_target="InvertDiagBlocksLowerTriangular" | custom-call | tf_op jit(solution)/shard_map/jit(cholesky)/cholesky | solution.py:62
  101.7 23.5 %custom-call.66 = f32[2,128,128]{2,1,0:T(8,128)S(1)} custom-call(f32[2,128,128]{2,1,0:T(8,128)S(1)} %cholesky.535), custom_call_target="Cholesky" | custom-call | tf_op jit(solution)/shard_map/jit(cholesky)/cholesky | solution.py:62
  125.2 19.8 %custom-call.67 = f32[2,1,128,128]{2,3,1,0:T(8,128)S(1)} custom-call(f32[2,1,128,128]{3,2,1,0:T(8,128)S(1)} %get-tuple-element.105), custom_call_target="InvertDiagBlocksLowerTriangular" | custom-call | tf_op jit(solution)/shard_map/jit(cholesky)/cholesky | solution.py:62
  147.0 23.5 %custom-call.68 = f32[2,128,128]{2,1,0:T(8,128)S(1)} custom-call(f32[2,128,128]{2,1,0:T(8,128)S(1)} %cholesky.540), custom_call_target="Cholesky" | custom-call | tf_op jit(solution)/shard_map/jit(cholesky)/cholesky | solution.py:62
  170.5 19.7 %custom-call.69 = f32[2,1,128,128]{2,3,1,0:T(8,128)S(1)} custom-call(f32[2,1,128,128]{3,2,1,0:T(8,128)S(1)} %get-tuple-element.103), custom_call_target="InvertDiagBlocksLowerTriangular" | custom-call | tf_op jit(solution)/shard_map/jit(cholesky)/cholesky | solution.py:62
  192.0 23.7 %custom-call.70 = f32[2,128,128]{2,1,0:T(8,128)S(1)} custom-call(f32[2,128,128]{2,1,0:T(8,128)S(1)} %convolution_subtract_fusion.7), custom_call_target="Cholesky" | custom-call | tf_op jit(solution)/shard_map/jit(cholesky)/cholesky | solution.py:62
  216.7 8.0 while.6
  224.7 39.3 %custom-call.78 = f32[4,128,128]{1,2,0:T(8,128)S(1)} custom-call(f32[4,128,128]{2,1,0:T(8,128)S(1)} %get-tuple-element.26), custom_call_target="InvertDiagBlocksLowerTriangular" | custom-call | tf_op jit(solution)/shard_map/triangular_solve/custom-call.14 | solution.py:41
  264.1 8.1 while.7
  272.2 39.7 %custom-call.79 = f32[4,128,128]{1,2,0:T(8,128)S(1)} custom-call(f32[4,128,128]{2,1,0:T(8,128)S(1)} %get-tuple-element.27), custom_call_target="InvertDiagBlocksLowerTriangular" | custom-call | tf_op jit(solution)/shard_map/triangular_solve/custom-call.14 | solution.py:41
  317.6 38.1 %all-gather.4.cloned.1.call-done = bf16[1024,1024]{0,1:T(8,128)(2,1)} async-done(((bf16[128,1024]{0,1:T(8,128)(2,1)}), bf16[1024,1024]{0,1:T(8,128)(2,1)}) %all-gather.4.cloned.1.call-update) | async-done | bytes 2097168 | tf_op jit(solution)/shard_map/all_gather | solution.py:77
  357.3 108.4 %all-reduce.6.cloned.1.call-done = bf16[1024,1024]{0,1:T(8,128)(2,1)} async-done(((bf16[1024,1024]{0,1:T(8,128)(2,1)}), bf16[1024,1024]{0,1:T(8,128)(2,1)}) %all-reduce.6.cloned.1.call-update) | async-done | bytes 2097168 | tf_op jit(solution)/shard_map/psum | solution.py:14
  465.7 5.3 negate_convert_fusion
  471.1 32.3 %reduce-scatter.3.cloned.1.call-done = bf16[256,1024]{0,1:T(8,128)(2,1)} async-done(((bf16[1024,1024]{0,1:T(8,128)(2,1)}), bf16[256,1024]{0,1:T(8,128)(2,1)}) %reduce-scatter.3.cloned.1.call-update) | async-done | bytes 524304 | tf_op jit(solution)/shard_map/reduce_scatter | solution.py:82
  510.0 29.9 %all-gather.6.cloned.1.call-done = bf16[1024,1024]{0,1:T(8,128)(2,1)} async-done(((bf16[256,1024]{0,1:T(8,128)(2,1)}), bf16[1024,1024]{0,1:T(8,128)(2,1)}) %all-gather.6.cloned.1.call-update) | async-done | bytes 2097168 | tf_op jit(solution)/shard_map/all_gather | solution.py:85
  547.9 186.4 %all-reduce.8.cloned.1.call-done = f32[512,512]{0,1:T(8,128)} async-done(((f32[512,512]{0,1:T(8,128)}), f32[512,512]{0,1:T(8,128)}) %all-reduce.8.cloned.1.call-update) | async-done | bytes 1048592 | tf_op jit(solution)/shard_map/psum | solution.py:14
  736.2 11.7 %cholesky.467 = f32[128,128]{1,0:T(8,128)S(1)} custom-call(f32[128,128]{1,0:T(8,128)S(1)} %cholesky.544), custom_call_target="Cholesky" | custom-call | tf_op jit(solution)/shard_map/jit(cholesky)/cholesky | solution.py:94
  748.0 9.8 custom-call.71
  758.7 11.7 %cholesky.483 = f32[128,128]{1,0:T(8,128)S(1)} custom-call(f32[128,128]{1,0:T(8,128)S(1)} %cholesky.548), custom_call_target="Cholesky" | custom-call | tf_op jit(solution)/shard_map/jit(cholesky)/cholesky | solution.py:94
  770.5 10.0 custom-call.72
  781.7 11.7 %cholesky.504 = f32[128,128]{1,0:T(8,128)S(1)} custom-call(f32[128,128]{1,0:T(8,128)S(1)} %cholesky.553), custom_call_target="Cholesky" | custom-call | tf_op jit(solution)/shard_map/jit(cholesky)/cholesky | solution.py:94
  793.6 9.8 custom-call.73
  804.2 11.7 %cholesky.521 = f32[128,128]{1,0:T(8,128)S(1)} custom-call(f32[128,128]{1,0:T(8,128)S(1)} %convolution_subtract_fusion.12), custom_call_target="Cholesky" | custom-call | tf_op jit(solution)/shard_map/jit(cholesky)/cholesky | solution.py:94
  821.4 8.6 while.5
  830.0 39.3 %custom-call.74 = f32[4,128,128]{1,2,0:T(8,128)S(1)} custom-call(f32[4,128,128]{2,1,0:T(8,128)S(1)} %get-tuple-element.19), custom_call_target="InvertDiagBlocksLowerTriangular" | custom-call | tf_op jit(solution)/shard_map/triangular_solve | solution.py:41
  887.8 99.3 %all-reduce.10.cloned.1.call-done = f32[1024,512]{0,1:T(8,128)} async-done(((f32[1024,512]{0,1:T(8,128)}), f32[1024,512]{0,1:T(8,128)}) %all-reduce.10.cloned.1.call-update) | async-done | bytes 2097168 | tf_op jit(solution)/shard_map/psum | solution.py:14
  987.1 5.7 convolution_subtract_fusion
  992.8 5.0 fusion
  1000.3 5.3 copy.101
  (193 shorter events, 91.2 us)
Async XLA Ops:
  7.2 15.5 %copy-start.11 = (s32[1,2,8]{2,1,0:T(2,128)S(1)}, s32[1,2,8]{2,1,0:T(2,128)}, u32[]{:S(2)}) copy-start(s32[1,2,8]{2,1,0:T(2,128)} %param.9) | copy-start | bytes 196
  7.2 15.7 %copy-start.10 = (bf16[1,128,1024]{2,1,0:T(8,128)(2,1)S(1)}, bf16[1,128,1024]{2,1,0:T(8,128)(2,1)}, u32[]{:S(2)}) copy-start(bf16[1,128,1024]{2,1,0:T(8,128)(2,1)} %param.7) | copy-start | bytes 786436
  9.1 40.9 %all-to-all-start = ((bf16[64,1,2,512,8]{3,4,2,1,0:T(8,128)(2,1)}), bf16[64,1,2,512,8]{3,4,2,1,0:T(8,128)(2,1)S(1)}, u32[]{:S(2)}, u32[]{:S(2)}) async-start(bf16[64,1,2,512,8]{3,4,2,1,0:T(8,128)(2,1)} %stack.2), calls=%async_computation | async-start | bytes 2097152 | tf_op jit(solution)/shard_map/all_to_all | solution.py:54
  22.1 333.6 %all-gather.4.cloned.1.call-start = ((), (), s32[]{:S(2)}) async-start(), calls=%async_computation.3 | async-start | bytes 2359296 | tf_op jit(solution)/shard_map/all_gather | solution.py:77
  53.9 1.3 copy-start.4
  216.6 95.3 %copy-start.9 = (f32[128,512]{1,0:T(8,128)S(1)}, f32[128,512]{1,0:T(8,128)}, u32[]{:S(2)}) copy-start(f32[128,512]{1,0:T(8,128)} %get-tuple-element.100) | copy-start | bytes 786436
  216.7 97.7 %copy-start.8 = (f32[128,512]{1,0:T(8,128)S(1)}, f32[128,512]{1,0:T(8,128)}, u32[]{:S(2)}) copy-start(f32[128,512]{1,0:T(8,128)} %get-tuple-element.101) | copy-start | bytes 786436
  317.5 148.2 %all-reduce.6.cloned.1.call-start = ((), (), s32[]{:S(2)}) async-start(), calls=%async_computation.4 | async-start | bytes 4194304 | tf_op jit(solution)/shard_map/psum | solution.py:14
  357.2 108.5 %copy-start.7 = (bf16[1024,1024]{0,1:T(8,128)(2,1)S(1)}, bf16[1024,1024]{0,1:T(8,128)(2,1)}, u32[]{:S(2)}) copy-start(bf16[1024,1024]{0,1:T(8,128)(2,1)} %all-gather.4.cloned.1.call-done) | copy-start | bytes 6291460
  357.2 146.1 %reduce-scatter.3.cloned.1.call-start = ((), (), s32[]{:S(2)}) async-start(), calls=%async_computation.5 | async-start | bytes 2621440 | tf_op jit(solution)/shard_map/reduce_scatter | solution.py:82
  471.0 69.0 %all-gather.6.cloned.1.call-start = ((), (), s32[]{:S(2)}) async-start(), calls=%async_computation.6 | async-start | bytes 2621440 | tf_op jit(solution)/shard_map/all_gather | solution.py:85
  503.3 230.9 %all-reduce.8.cloned.1.call-start = ((), (), s32[]{:S(2)}) async-start(), calls=%async_computation.9 | async-start | bytes 2097152 | tf_op jit(solution)/shard_map/psum | solution.py:14
  542.0 2.7 copy-start
  544.7 1.3 copy-start.2
  547.1 233.9 %reduce-scatter.5.cloned.1.call-start = ((), (), s32[]{:S(2)}) async-start(), calls=%async_computation.7 | async-start | bytes 2359296 | tf_op jit(solution)/shard_map/reduce_scatter | solution.py:27
  547.7 321.7 %all-gather.8.cloned.1.call-start = ((), (), s32[]{:S(2)}) async-start(), calls=%async_computation.8 | async-start | bytes 2359296 | tf_op jit(solution)/shard_map/all_gather | solution.py:28
  734.3 1.7 copy-start.5
  781.0 206.1 %all-reduce.10.cloned.1.call-start = ((), (), s32[]{:S(2)}) async-start(), calls=%async_computation.10 | async-start | bytes 4194304 | tf_op jit(solution)/shard_map/psum | solution.py:14
  869.3 4.1 copy-start.6
  987.1 5.7 copy-start.1
  987.1 5.7 copy-start.3
Sparse Core Ops, SparseCore 0:
  317.6 38.0 all-gather.3
  358.9 106.6 all-reduce.5
  471.1 32.1 reduce-scatter.2
  505.0 34.9 all-gather.5
  547.2 187.0 all-reduce.7
  736.7 41.5 reduce-scatter.4
  781.2 41.0 all-gather.7
  878.8 108.2 all-reduce.9
